TPU v7x, 32 devices: a whole 2x2x4 slice. The times are simulated.
32 devices in a mesh: dp: 2 (over x), crop: 4 (over y, core), tensor: 4 (over z).
Axes of the slice: x: 2, y: 2, z: 4, core: 2. Of those that a mesh axis runs over, the one named last changes fastest.
Arguments:
- hidden_a: bfloat16 [512, 8192], P('crop', 'dp'), as said below
- hidden_b: bfloat16 [512, 8192], P('crop', 'dp'), as said below
- weight: bfloat16 [8192, 8192], P('dp', 'tensor')
Outputs:
- weight_grad: float32 [8192, 8192], P(('dp', 'crop'), 'tensor')
Inputs may be any that keep to these rules, and one draw needn't show every extreme that they name: `hidden_a`: nonnegative entries. `hidden_b`: nonnegative entries.
All inputs are finite; a program needn't handle non-finite values.
Results may differ from a plain program's by a relative error of at most 0.0015.
Values may be sent and summed in bfloat16 or wider, within the bound.
A program may use at most 128 MiB of HBM per device.

v0:
```python
import jax
import jax.numpy as jnp
from jax import lax
from jax.sharding import PartitionSpec as P

epsilon = 0.0001


def body(hidden_a, hidden_b, weight):
    group_size = lax.axis_size(("dp", "crop"))
    data_count = lax.axis_size("dp")
    block_rows = hidden_a.shape[0]
    local_rows = block_rows // data_count
    total_rows = local_rows * group_size
    left_part = jnp.dot(hidden_a, weight, preferred_element_type=jnp.float32)
    right_part = jnp.dot(hidden_b, weight, preferred_element_type=jnp.float32)
    joined = lax.psum_scatter(
        jnp.stack([left_part, right_part], axis=1), "dp", scatter_dimension=0, tiled=True
    ).astype(jnp.bfloat16)
    stacked = jnp.stack([joined[:, 0, :], joined[:, 1, :]]).astype(jnp.float32)
    col_means = lax.psum(jnp.sum(stacked, axis=1), ("dp", "crop")) / total_rows
    centered = stacked - col_means[:, None, :]
    spread = lax.psum(jnp.sum(centered * centered, axis=1), ("dp", "crop"))
    deviation = jnp.sqrt(spread / (total_rows - 1.0) + epsilon)
    rounded = centered.astype(jnp.bfloat16)
    everyone = lax.all_gather(rounded, ("dp", "crop"), axis=1, tiled=True)
    gram = jnp.einsum("vrf,vbf->vrb", rounded, everyone, preferred_element_type=jnp.float32)
    gram = lax.psum(gram, "tensor")
    gram_low = gram.astype(jnp.bfloat16)
    products = jnp.einsum("vrb,vbf->vrf", gram_low, everyone, preferred_element_type=jnp.float32)
    hinge_rate = jnp.where(deviation < 1.0, 25.0 / ((total_rows - 1.0) * deviation), 0.0)[
        :, None, :
    ]
    differ = stacked[0] - stacked[1]
    pull_term = jnp.stack([differ, -differ]) * (50.0 / total_rows)
    cov_scale = 4.0 / (total_rows - 1.0) ** 2
    row_grads = (
        pull_term - hinge_rate * centered + cov_scale * (products - centered * spread[:, None, :])
    )
    row_grads = row_grads.astype(jnp.bfloat16)
    block_grads = lax.all_gather(row_grads, "dp", axis=1, tiled=True)
    across = (((0,), (0,)), ((), ()))
    left_part = lax.dot_general(
        hidden_a, block_grads[0], across, preferred_element_type=jnp.float32
    )
    right_part = lax.dot_general(
        hidden_b, block_grads[1], across, preferred_element_type=jnp.float32
    )
    return lax.psum_scatter(left_part + right_part, "crop", scatter_dimension=0, tiled=True)


def solution(mesh):
    placed = (P("crop", "dp"), P("crop", "dp"), P("dp", "tensor"))
    return jax.shard_map(
        body, mesh=mesh, in_specs=placed, out_specs=P(("dp", "crop"), "tensor"), check_vma=False
    )
```

profile of v0, /device:TPU:0, one launch (start us, length us, event | category | flops | bytes accessed | tf_op | source)
XLA Modules:
  0.0 458.1 jit_solution(6418926525455714938)
XLA Ops:
  6.5 1.2 copy-done
  7.8 8.2 %convolution_bitcast_fusion.1 = f32[128,1,2048]{2,0,1:T(8,128)S(1)} fusion(bf16[128,4096]{1,0:T(8,128)(2,1)S(1)} %copy-done, bf16[4096,2048]{1,0:T(8,128)(2,1)} %param.5), kind=kOutput, calls=%fused_computation.5 | convolution fusion | flops 2147483648 | bytes 18874368 | tf_op jit(solution)/shard_map/dot_general | solution.py:15
  16.0 2.4 copy-done.2
  18.4 2.4 convolution_bitcast_fusion
  20.8 1.5 pad_maximum_fusion
  22.3 34.7 %reduce-scatter.3.cloned.1.call-done = f32[64,2,2048]{2,0,1:T(8,128)} async-done(((f32[128,2,2048]{2,0,1:T(8,128)}), f32[64,2,2048]{2,0,1:T(8,128)}) %reduce-scatter.3.cloned.1.call-update) | async-done | bytes 1048592 | tf_op jit(solution)/shard_map/reduce_scatter | solution.py:17
  57.1 1.3 convert_element_type.15
  58.4 0.1 convert_reduce_fusion
  58.5 22.9 %psum.21 = f32[2,2048]{1,0:T(2,128)S(1)} all-reduce(f32[2,2048]{1,0:T(2,128)S(1)} %convert_reduce_fusion), channel_id=1, replica_groups=mesh['dp'=2,'crop'=4,'tensor'=4] {'dp','crop'}, use_global_device_ids=true, to_apply=%region_2.0 | all-reduce | flops 4096 | bytes 32768 | tf_op jit(solution)/shard_map/psum | solution.py:21
  81.5 1.0 multiply_reduce_fusion
  82.5 22.7 %psum.22 = f32[2,2048]{1,0:T(2,128)S(1)} all-reduce(f32[2,2048]{1,0:T(2,128)S(1)} %get-tuple-element.7), channel_id=1, replica_groups=mesh['dp'=2,'crop'=4,'tensor'=4] {'dp','crop'}, use_global_device_ids=true, to_apply=%region_4.0 | all-reduce | flops 4096 | bytes 32768 | tf_op jit(solution)/shard_map/psum | solution.py:23
  105.3 0.5 copy-done.5
  105.8 0.6 compare_select_fusion
  106.4 0.9 fusion.7
  107.3 12.0 %all-gather.3.cloned.1.call-done = bf16[2,512,2048]{2,1,0:T(8,128)(2,1)} async-done(((bf16[2,64,2048]{2,1,0:T(8,128)(2,1)}), bf16[2,512,2048]{2,1,0:T(8,128)(2,1)}) %all-gather.3.cloned.1.call-update) | async-done | bytes 4194320 | tf_op jit(solution)/shard_map/all_gather | solution.py:26
  119.3 3.7 fusion.8
  123.1 24.7 %all-reduce.1 = bf16[2,64,512]{2,1,0:T(8,128)(2,1)S(1)} all-reduce(f32[2,64,512]{2,1,0:T(8,128)S(1)} %fusion.8), channel_id=1, replica_groups=mesh['dp'=2,'crop'=4,'tensor'=4] {'tensor'}, use_global_device_ids=true, to_apply=%region_5.0 | all-reduce | flops 65536 | bytes 393216 | tf_op jit(solution)/shard_map/psum | solution.py:28
  147.7 4.2 fusion.2
  152.0 0.2 reduce-scatter.5.cloned.1.call-start
  152.2 18.8 %all-gather.5.cloned.1.call-done = bf16[2,128,2048]{2,1,0:T(8,128)(2,1)} async-done(((bf16[2,64,2048]{2,1,0:T(8,128)(2,1)}), bf16[2,128,2048]{2,1,0:T(8,128)(2,1)}) %all-gather.5.cloned.1.call-update) | async-done | bytes 1048592 | tf_op jit(solution)/shard_map/all_gather | solution.py:41
  171.0 14.3 %fusion.4 = f32[2048,4096]{1,0:T(8,128)} fusion(bf16[128,4096]{1,0:T(8,128)(2,1)S(1)} %copy-done, bf16[2,128,2048]{2,1,0:T(8,128)(2,1)} %all-gather.5.cloned.1.call-done), kind=kOutput, calls=%fused_computation.15 | convolution fusion | flops 2147483648 | bytes 35127296 | tf_op jit(solution)/shard_map/dot_general | solution.py:43
  185.3 24.8 %add_bitcast_fusion = f32[4096,2048]{0,1:T(8,128)} fusion(f32[2048,4096]{1,0:T(8,128)} %fusion.4, bf16[128,4096]{1,0:T(8,128)(2,1)S(1)} %copy-done.3, bf16[2,128,2048]{2,1,0:T(8,128)(2,1)S(1)} %copy-done.4), kind=kOutput, calls=%fused_computation | convolution fusion | flops 2155872256 | bytes 68681728 | tf_op jit(solution)/shard_map/dot_general | solution.py:46
  210.1 232.3 %reduce-scatter.5.cloned.1.call-done = f32[1024,2048]{0,1:T(8,128)} async-done(((f32[4096,2048]{0,1:T(8,128)}), f32[1024,2048]{0,1:T(8,128)}) %reduce-scatter.5.cloned.1.call-update) | async-done | bytes 8388624 | tf_op jit(solution)/shard_map/reduce_scatter | solution.py:49
  442.4 9.1 %copy.4 = f32[1024,2048]{1,0:T(8,128)} copy(f32[1024,2048]{0,1:T(8,128)} %reduce-scatter.5.cloned.1.call-done) | data formatting | bytes 16777216 | tf_op jit(solution)/shard_map/reduce_scatter | solution.py:49
  (19 shorter events, 0.3 us)
Async XLA Ops:
  6.5 1.2 copy-start
  6.5 9.5 %copy-start.3 = (bf16[128,4096]{1,0:T(8,128)(2,1)S(1)}, bf16[128,4096]{1,0:T(8,128)(2,1)}, u32[]{:S(2)}) copy-start(bf16[128,4096]{1,0:T(8,128)(2,1)} %param.4) | copy-start | bytes 3145732
  6.5 50.5 %reduce-scatter.3.cloned.1.call-start = ((), (), s32[]{:S(2)}) async-start(), calls=%async_computation.2 | async-start | bytes 3145728 | tf_op jit(solution)/shard_map/reduce_scatter | solution.py:17
  7.8 10.6 %copy-start.2 = (bf16[4096,2048]{1,0:T(8,128)(2,1)S(1)}, bf16[4096,2048]{1,0:T(8,128)(2,1)}, u32[]{:S(2)}) copy-start(bf16[4096,2048]{1,0:T(8,128)(2,1)} %param.5) | copy-start | bytes 50331652
  22.3 97.0 %all-gather.3.cloned.1.call-start = ((), (), s32[]{:S(2)}) async-start(), calls=%async_computation.3 | async-start | bytes 4718592 | tf_op jit(solution)/shard_map/all_gather | solution.py:26
  82.4 88.5 %all-gather.5.cloned.1.call-start = ((), (), s32[]{:S(2)}) async-start(), calls=%async_computation.4 | async-start | bytes 1572864 | tf_op jit(solution)/shard_map/all_gather | solution.py:41
  105.2 0.6 copy-start.5
  152.0 290.4 %reduce-scatter.5.cloned.1.call-start = ((), (), s32[]{:S(2)}) async-start(), calls=%async_computation.5 | async-start | bytes 41943040 | tf_op jit(solution)/shard_map/reduce_scatter | solution.py:49
  171.0 14.3 %copy-start.4 = (bf16[2,128,2048]{2,1,0:T(8,128)(2,1)S(1)}, bf16[2,128,2048]{2,1,0:T(8,128)(2,1)}, u32[]{:S(2)}) copy-start(bf16[2,128,2048]{2,1,0:T(8,128)(2,1)} %all-gather.5.cloned.1.call-done) | copy-start | bytes 3145732
  210.1 241.5 %copy-start.1 = (bf16[128,4096]{1,0:T(8,128)(2,1)S(1)}, bf16[128,4096]{1,0:T(8,128)(2,1)}, u32[]{:S(2)}) copy-start(bf16[128,4096]{1,0:T(8,128)(2,1)} %param.3) | copy-start | bytes 3145732
Sparse Core Ops, SparseCore 0:
  22.4 34.6 reduce-scatter.2
  82.6 36.6 all-gather.2
  152.1 18.8 all-gather.4
  210.2 232.1 reduce-scatter.4
where the time goes:
time: 458 us
  waiting for transfers between devices  298 us (65%)
  blocking collectives  70.3 us (15%)
  matrix products  57.7 us (13%)
  local copies, waits for them, and re-layouts  13.3 us (3%)
  between operations  13.2 us (3%)
  other arithmetic  5.43 us (1%)
    reduce_scatter x1, waiting for transfers between devices, body(): lax.psum_scatter(left_part + right_part, 'crop', scatter_dimension=0, til...  232 us
    reduce_scatter x1, waiting for transfers between devices, body(): lax.psum_scatter(jnp.stack([left_part, right_part], axis=1), 'dp', scatte...  34.7 us
    dot_general x1, matrix products, body(): lax.dot_general(hidden_b, block_grads[1], across, preferred_element_type=...  24.8 us
    psum x1, blocking collectives, body(): gram = lax.psum(gram, 'tensor')  24.7 us
    psum x1, blocking collectives, body(): col_means = lax.psum(jnp.sum(stacked, axis=1), ('dp', 'crop')) / total_rows  22.9 us
    psum x1, blocking collectives, body(): spread = lax.psum(jnp.sum(centered * centered, axis=1), ('dp', 'crop'))  22.7 us
    all_gather x1, waiting for transfers between devices, body(): block_grads = lax.all_gather(row_grads, 'dp', axis=1, tiled=True)  18.8 us
    dot_general x1, matrix products, body(): lax.dot_general(hidden_a, block_grads[0], across, preferred_element_type=...  14.3 us
  transfers between devices with their start and end apart: 4, of which 4 were waited for; matrix products, arithmetic and copies ran while one was open for 0% of the time, Pallas kernels for 0%

commit v1 on v0

--- a/solution.py
+++ b/solution.py
@@ -4,6 +4,11 @@
 from jax.sharding import PartitionSpec as P
 
 epsilon = 0.0001
+
+
+def add_all(array, axis):
+    parts = lax.all_gather(array, axis)
+    return jnp.sum(parts, axis=0)
 
 
 def body(hidden_a, hidden_b, weight):
@@ -18,7 +23,7 @@
         jnp.stack([left_part, right_part], axis=1), "dp", scatter_dimension=0, tiled=True
     ).astype(jnp.bfloat16)
     stacked = jnp.stack([joined[:, 0, :], joined[:, 1, :]]).astype(jnp.float32)
-    col_means = lax.psum(jnp.sum(stacked, axis=1), ("dp", "crop")) / total_rows
+    col_means = add_all(jnp.sum(stacked, axis=1), ("dp", "crop")) / total_rows
     centered = stacked - col_means[:, None, :]
     spread = lax.psum(jnp.sum(centered * centered, axis=1), ("dp", "crop"))
     deviation = jnp.sqrt(spread / (total_rows - 1.0) + epsilon)

time: 458 us -> 445 us (0.972)
  blocking collectives: 70.3 us -> 57.9 us
    psum x1 -> x0, blocking collectives: 22.9 us -> none  [body(): col_means = lax.psum(jnp.sum(stacked, axis=1), ('dp', 'crop')) / total_rows]
    all_gather x0 -> x1, blocking collectives: none -> 9.19 us  [add_all(): parts = lax.all_gather(array, axis)]
where the time goes in v1:
time: 445 us; the launch traced here: 444 us
  waiting for transfers between devices  297 us (67%)
  blocking collectives  57.9 us (13%)
  matrix products  57.7 us (13%)
  local copies, waits for them, and re-layouts  13.3 us (3%)
  between operations  13.2 us (3%)
  other arithmetic  5.48 us (1%)
    reduce_scatter x1, waiting for transfers between devices, body(): lax.psum_scatter(left_part + right_part, 'crop', scatter_dimension=0, til...  232 us
    reduce_scatter x1, waiting for transfers between devices, body(): lax.psum_scatter(jnp.stack([left_part, right_part], axis=1), 'dp', scatte...  34.7 us
    dot_general x1, matrix products, body(): lax.dot_general(hidden_b, block_grads[1], across, preferred_element_type=...  24.8 us
    psum x1, blocking collectives, body(): gram = lax.psum(gram, 'tensor')  24.7 us
    psum x1, blocking collectives, body(): spread = lax.psum(jnp.sum(centered * centered, axis=1), ('dp', 'crop'))  24.1 us
    all_gather x1, waiting for transfers between devices, body(): block_grads = lax.all_gather(row_grads, 'dp', axis=1, tiled=True)  18.7 us
    dot_general x1, matrix products, body(): lax.dot_general(hidden_a, block_grads[0], across, preferred_element_type=...  14.3 us
    all_gather x1, waiting for transfers between devices, body(): everyone = lax.all_gather(rounded, ('dp', 'crop'), axis=1, tiled=True)  10.7 us
  transfers between devices with their start and end apart: 4, of which 4 were waited for; matrix products, arithmetic and copies ran while one was open for 0% of the time, Pallas kernels for 0%

profile of v1, /device:TPU:0, one launch (start us, length us, event | category | flops | bytes accessed | tf_op | source)
XLA Modules:
  0.0 444.4 jit_solution(5862508707806952413)
XLA Ops:
  6.5 1.2 copy-done
  7.8 8.2 %convolution_bitcast_fusion.1 = f32[128,1,2048]{2,0,1:T(8,128)S(1)} fusion(bf16[128,4096]{1,0:T(8,128)(2,1)S(1)} %copy-done, bf16[4096,2048]{1,0:T(8,128)(2,1)} %param.5), kind=kOutput, calls=%fused_computation.5 | convolution fusion | flops 2147483648 | bytes 18874368 | tf_op jit(solution)/shard_map/dot_general | solution.py:20
  16.0 2.4 copy-done.2
  18.4 2.4 convolution_bitcast_fusion
  20.8 1.5 pad_maximum_fusion
  22.3 34.7 %reduce-scatter.3.cloned.1.call-done = f32[64,2,2048]{2,0,1:T(8,128)} async-done(((f32[128,2,2048]{2,0,1:T(8,128)}), f32[64,2,2048]{2,0,1:T(8,128)}) %reduce-scatter.3.cloned.1.call-update) | async-done | bytes 1048592 | tf_op jit(solution)/shard_map/reduce_scatter | solution.py:22
  57.1 1.3 convert_element_type.15
  58.4 0.1 convert_reduce_fusion
  58.5 9.2 %all-gather.1 = f32[8,2,2048]{2,1,0:T(2,128)S(1)} all-gather(f32[1,2,2048]{2,1,0:T(2,128)S(1)} %bitcast.27), channel_id=2, replica_groups=mesh['dp'=2,'crop'=4,'tensor'=4] {'dp','crop'}, dimensions={0}, use_global_device_ids=true | all-gather | bytes 147456 | tf_op jit(solution)/shard_map/all_gather | solution.py:10
  67.8 1.0 multiply_reduce_fusion
  68.8 24.1 %psum.14 = f32[2,2048]{1,0:T(2,128)S(1)} all-reduce(f32[2,2048]{1,0:T(2,128)S(1)} %get-tuple-element.7), channel_id=1, replica_groups=mesh['dp'=2,'crop'=4,'tensor'=4] {'dp','crop'}, use_global_device_ids=true, to_apply=%region_4.0 | all-reduce | flops 4096 | bytes 32768 | tf_op jit(solution)/shard_map/psum | solution.py:28
  92.9 0.5 copy-done.5
  93.5 0.6 compare_select_fusion
  94.1 0.9 fusion.7
  95.0 10.7 %all-gather.5.cloned.1.call-done = bf16[2,512,2048]{2,1,0:T(8,128)(2,1)} async-done(((bf16[2,64,2048]{2,1,0:T(8,128)(2,1)}), bf16[2,512,2048]{2,1,0:T(8,128)(2,1)}) %all-gather.5.cloned.1.call-update) | async-done | bytes 4194320 | tf_op jit(solution)/shard_map/all_gather | solution.py:31
  105.7 3.7 fusion.8
  109.4 24.7 %all-reduce.1 = bf16[2,64,512]{2,1,0:T(8,128)(2,1)S(1)} all-reduce(f32[2,64,512]{2,1,0:T(8,128)S(1)} %fusion.8), channel_id=1, replica_groups=mesh['dp'=2,'crop'=4,'tensor'=4] {'tensor'}, use_global_device_ids=true, to_apply=%region_5.0 | all-reduce | flops 65536 | bytes 393216 | tf_op jit(solution)/shard_map/psum | solution.py:33
  134.1 4.2 fusion.2
  138.4 0.2 reduce-scatter.5.cloned.1.call-start
  138.6 18.7 %all-gather.7.cloned.1.call-done = bf16[2,128,2048]{2,1,0:T(8,128)(2,1)} async-done(((bf16[2,64,2048]{2,1,0:T(8,128)(2,1)}), bf16[2,128,2048]{2,1,0:T(8,128)(2,1)}) %all-gather.7.cloned.1.call-update) | async-done | bytes 1048592 | tf_op jit(solution)/shard_map/all_gather | solution.py:46
  157.3 14.3 %fusion.4 = f32[2048,4096]{1,0:T(8,128)} fusion(bf16[128,4096]{1,0:T(8,128)(2,1)S(1)} %copy-done, bf16[2,128,2048]{2,1,0:T(8,128)(2,1)} %all-gather.7.cloned.1.call-done), kind=kOutput, calls=%fused_computation.15 | convolution fusion | flops 2147483648 | bytes 35127296 | tf_op jit(solution)/shard_map/dot_general | solution.py:48
  171.6 24.8 %add_bitcast_fusion = f32[4096,2048]{0,1:T(8,128)} fusion(f32[2048,4096]{1,0:T(8,128)} %fusion.4, bf16[128,4096]{1,0:T(8,128)(2,1)S(1)} %copy-done.3, bf16[2,128,2048]{2,1,0:T(8,128)(2,1)S(1)} %copy-done.4), kind=kOutput, calls=%fused_computation | convolution fusion | flops 2155872256 | bytes 68681728 | tf_op jit(solution)/shard_map/dot_general | solution.py:51
  196.4 232.3 %reduce-scatter.5.cloned.1.call-done = f32[1024,2048]{0,1:T(8,128)} async-done(((f32[4096,2048]{0,1:T(8,128)}), f32[1024,2048]{0,1:T(8,128)}) %reduce-scatter.5.cloned.1.call-update) | async-done | bytes 8388624 | tf_op jit(solution)/shard_map/reduce_scatter | solution.py:54
  428.8 9.1 %copy.5 = f32[1024,2048]{1,0:T(8,128)} copy(f32[1024,2048]{0,1:T(8,128)} %reduce-scatter.5.cloned.1.call-done) | data formatting | bytes 16777216 | tf_op jit(solution)/shard_map/reduce_scatter | solution.py:54
  (20 shorter events, 0.3 us)
Async XLA Ops:
  6.5 1.2 copy-start
  6.5 9.5 %copy-start.3 = (bf16[128,4096]{1,0:T(8,128)(2,1)S(1)}, bf16[128,4096]{1,0:T(8,128)(2,1)}, u32[]{:S(2)}) copy-start(bf16[128,4096]{1,0:T(8,128)(2,1)} %param.4) | copy-start | bytes 3145732
  6.5 50.5 %reduce-scatter.3.cloned.1.call-start = ((), (), s32[]{:S(2)}) async-start(), calls=%async_computation.2 | async-start | bytes 3145728 | tf_op jit(solution)/shard_map/reduce_scatter | solution.py:22
  7.8 10.6 %copy-start.2 = (bf16[4096,2048]{1,0:T(8,128)(2,1)S(1)}, bf16[4096,2048]{1,0:T(8,128)(2,1)}, u32[]{:S(2)}) copy-start(bf16[4096,2048]{1,0:T(8,128)(2,1)} %param.5) | copy-start | bytes 50331652
  22.3 83.4 %all-gather.5.cloned.1.call-start = ((), (), s32[]{:S(2)}) async-start(), calls=%async_computation.3 | async-start | bytes 4718592 | tf_op jit(solution)/shard_map/all_gather | solution.py:31
  68.8 88.6 %all-gather.7.cloned.1.call-start = ((), (), s32[]{:S(2)}) async-start(), calls=%async_computation.4 | async-start | bytes 1572864 | tf_op jit(solution)/shard_map/all_gather | solution.py:46
  92.9 0.6 copy-start.5
  138.4 290.4 %reduce-scatter.5.cloned.1.call-start = ((), (), s32[]{:S(2)}) async-start(), calls=%async_computation.5 | async-start | bytes 41943040 | tf_op jit(solution)/shard_map/reduce_scatter | solution.py:54
  157.3 14.3 %copy-start.4 = (bf16[2,128,2048]{2,1,0:T(8,128)(2,1)S(1)}, bf16[2,128,2048]{2,1,0:T(8,128)(2,1)}, u32[]{:S(2)}) copy-start(bf16[2,128,2048]{2,1,0:T(8,128)(2,1)} %all-gather.7.cloned.1.call-done) | copy-start | bytes 3145732
  196.4 241.5 %copy-start.1 = (bf16[128,4096]{1,0:T(8,128)(2,1)S(1)}, bf16[128,4096]{1,0:T(8,128)(2,1)}, u32[]{:S(2)}) copy-start(bf16[128,4096]{1,0:T(8,128)(2,1)} %param.3) | copy-start | bytes 3145732
Sparse Core Ops, SparseCore 0:
  22.4 34.6 reduce-scatter.2
  68.9 36.7 all-gather.4
  138.5 18.8 all-gather.6
  196.5 232.1 reduce-scatter.4
